TPU v7x, 32 devices: a whole 2x2x4 slice. The times are simulated.
32 devices in a mesh: clip: 4 (over x, core), tx: 4 (over z), ty: 2 (over y).
Axes of the slice: x: 2, y: 2, z: 4, core: 2. Of those that a mesh axis runs over, the one named last changes fastest.
Arguments:
- query_states: bfloat16 [32, 128, 1152], P(('clip', 'tx', 'ty')), parts along dimension 0, may hold values from -64 to 64
- key_states: bfloat16 [32, 128, 1152], P(('clip', 'tx', 'ty')), parts along dimension 0, may hold values from -24 to 24
- value_states: bfloat16 [32, 128, 1152], P(('clip', 'tx', 'ty')), parts along dimension 0, may hold values from -6 to 6
- grad_output: bfloat16 [32, 128, 1152], P(('clip', 'tx', 'ty')), parts along dimension 0, may hold values from -6 to 6
- branch_gate: float32 [4608], P('clip'), parts along dimension 0, may hold values from 0.1 to 1.9
- out_weight: bfloat16 [1152, 1152], P('tx'), may hold values from -0.1875 to 0.1875
Outputs:
- query_grad: bfloat16 [32, 128, 1152], P(('clip', 'tx', 'ty')), parts along dimension 0
- key_grad: bfloat16 [32, 128, 1152], P(('clip', 'tx', 'ty')), parts along dimension 0
- value_grad: bfloat16 [32, 128, 1152], P(('clip', 'tx', 'ty')), parts along dimension 0
- gate_grad: float32 [4608], P('clip'), parts along dimension 0
There are 4 independent parts, one for each index of `clip`. A program takes and returns all parts, laid end to end along the dimension named above; an argument that names none is the same for every part. Nothing has to cross between parts.
All inputs are finite; a program needn't handle non-finite values.
Results may differ from a plain program's by a relative error of at most 0.025.
Values may be sent and summed in bfloat16 or wider, within the bound.
A program may use at most 64 MiB of HBM per device.

v0:
```python
import jax
import jax.numpy as jnp
from jax import lax
from jax.sharding import PartitionSpec as P

HEAD_DIM = 72


def shortened(x):

    def short(part):
        return part.astype(jnp.bfloat16) if part.dtype == jnp.float32 else part

    return jax.tree.map(short, x)


def attend_block(queries, keys_in, values_in, grads_in):
    frames, block_pos, block_width = queries.shape
    heads_here = block_width // HEAD_DIM
    shape4 = (frames, block_pos, heads_here, HEAD_DIM)
    q_four = queries.reshape(shape4)
    k_four = keys_in.reshape(shape4)
    v_four = values_in.reshape(shape4)
    g_four = grads_in.reshape(shape4)
    factor = HEAD_DIM ** (-0.5)
    scores = (
        jnp.einsum("fphd,gphd->phfg", q_four, k_four, preferred_element_type=jnp.float32) * factor
    )
    peak = jnp.max(scores, axis=-1, keepdims=True)
    expon = jnp.exp(scores - peak)
    probs = expon / jnp.sum(expon, axis=-1, keepdims=True)
    probs_b = probs.astype(jnp.bfloat16)
    attn_out = jnp.einsum(
        "phfg,gphd->fphd", probs_b, v_four, preferred_element_type=jnp.float32
    ).astype(jnp.bfloat16)
    value_grad = jnp.einsum(
        "phfg,fphd->gphd", probs_b, g_four, preferred_element_type=jnp.float32
    ).astype(jnp.bfloat16)
    dprobs = jnp.einsum("fphd,gphd->phfg", g_four, v_four, preferred_element_type=jnp.float32)
    delta = jnp.sum(g_four.astype(jnp.float32) * attn_out.astype(jnp.float32), axis=-1)
    delta = jnp.transpose(delta, (1, 2, 0))[..., None]
    dscores = (probs * (dprobs - delta) * factor).astype(jnp.bfloat16)
    query_grad = jnp.einsum(
        "phfg,gphd->fphd", dscores, k_four, preferred_element_type=jnp.float32
    ).astype(jnp.bfloat16)
    key_grad = jnp.einsum(
        "phfg,fphd->gphd", dscores, q_four, preferred_element_type=jnp.float32
    ).astype(jnp.bfloat16)
    flat = (frames, block_pos, block_width)
    return (
        query_grad.reshape(flat),
        key_grad.reshape(flat),
        value_grad.reshape(flat),
        attn_out.reshape(flat),
    )


def split_for_direct(array, across_x, across_y):
    positions, width = array.shape
    pieces = array.reshape(across_y, positions // across_y, across_x, width // across_x)
    pieces = jnp.transpose(pieces, (2, 0, 1, 3))
    return pieces.reshape(1, across_x * across_y, positions // across_y, width // across_x)


def join_from_direct(array, across_x, across_y):
    block_pos, block_width = (array.shape[2], array.shape[3])
    pieces = array.reshape(across_x, across_y, block_pos, block_width)
    pieces = jnp.transpose(pieces, (1, 2, 0, 3))
    return pieces.reshape(1, across_y * block_pos, across_x * block_width)


def per_device(query_states, key_states, value_states, grad_output, branch_gate, out_weight):
    across_x = lax.axis_size("tx")
    across_y = lax.axis_size("ty")
    devices_here = across_x * across_y
    positions = grad_output.shape[1]
    width = grad_output.shape[2]
    block_pos = positions // across_y
    block_width = width // across_x
    grad_rows = grad_output[0]
    gated = (grad_rows.astype(jnp.float32) * branch_gate).astype(jnp.bfloat16)
    d_attn = lax.dot_general(
        gated,
        lax.all_gather(out_weight, "tx", axis=0, tiled=True),
        (((1,), (1,)), ((), ())),
        preferred_element_type=jnp.float32,
    )
    d_attn = d_attn.astype(jnp.bfloat16)
    sources = (query_states[0], key_states[0], value_states[0], d_attn)
    prepared = tuple((split_for_direct(arr, across_x, across_y) for arr in sources))
    moved = jax.tree.map(
        lambda part, own: part.astype(own.dtype),
        lax.all_to_all(shortened(prepared), ("tx", "ty"), split_axis=1, concat_axis=0, tiled=True),
        prepared,
    )
    moved = tuple((arr.reshape(devices_here, block_pos, block_width) for arr in moved))
    results = attend_block(moved[0], moved[1], moved[2], moved[3])
    outgoing = tuple((arr.reshape(devices_here, 1, block_pos, block_width) for arr in results))
    returned = jax.tree.map(
        lambda part, own: part.astype(own.dtype),
        lax.all_to_all(shortened(outgoing), ("tx", "ty"), split_axis=0, concat_axis=1, tiled=True),
        outgoing,
    )
    returned = tuple((join_from_direct(arr, across_x, across_y) for arr in returned))
    query_grad, key_grad, value_grad, attn_frame = returned
    attn_rows = attn_frame[0]
    branch_out = jnp.dot(
        attn_rows,
        lax.all_gather(out_weight, "tx", axis=0, tiled=True),
        preferred_element_type=jnp.float32,
    )
    local_terms = jnp.sum(grad_rows.astype(jnp.float32) * branch_out, axis=0)
    gate_grad = lax.psum(local_terms, ("tx", "ty"))
    return (query_grad, key_grad, value_grad, gate_grad)


def solution(mesh):
    in_specs = (
        P(("clip", "tx", "ty"), None, None),
        P(("clip", "tx", "ty"), None, None),
        P(("clip", "tx", "ty"), None, None),
        P(("clip", "tx", "ty"), None, None),
        P("clip"),
        P("tx", None),
    )
    out_specs = (
        P(("clip", "tx", "ty"), None, None),
        P(("clip", "tx", "ty"), None, None),
        P(("clip", "tx", "ty"), None, None),
        P("clip"),
    )
    return jax.shard_map(
        per_device, mesh=mesh, in_specs=in_specs, out_specs=out_specs, check_vma=False
    )
```

profile of v0, /device:TPU:0, one launch (start us, length us, event | category | flops | bytes accessed | tf_op | source)
XLA Modules:
  0.0 204.5 jit_solution(13158037343326057094)
XLA Ops:
  7.2 0.7 all-gather.2.cloned.1.call-update
  7.9 1.3 reshape_squeeze.9
  9.2 0.8 copy.55
  10.1 7.4 %all-to-all-start = ((bf16[1,8,64,288]{3,2,0,1:T(8,128)(2,1)}), bf16[1,8,64,288]{3,2,0,1:T(8,128)(2,1)S(1)}, u32[]{:S(2)}, u32[]{:S(2)}) async-start(bf16[1,8,64,288]{3,2,0,1:T(8,128)(2,1)} %bitcast.2), calls=%async_computation | async-start | bytes 786432 | tf_op jit(solution)/shard_map/all_to_all | solution.py:93
  17.5 0.4 reshape_squeeze.10
  17.9 0.8 copy.57
  18.7 19.1 %all-to-all-done = bf16[1,8,64,288]{3,2,0,1:T(8,128)(2,1)S(1)} async-done(((bf16[1,8,64,288]{3,2,0,1:T(8,128)(2,1)}), bf16[1,8,64,288]{3,2,0,1:T(8,128)(2,1)S(1)}, u32[]{:S(2)}, u32[]{:S(2)}) %all-to-all-start) | async-done | bytes 294944 | tf_op jit(solution)/shard_map/all_to_all | solution.py:93
  37.8 6.1 %all-to-all-start.1 = ((bf16[1,8,64,288]{3,2,0,1:T(8,128)(2,1)}), bf16[1,8,64,288]{3,2,0,1:T(8,128)(2,1)S(1)}, u32[]{:S(2)}, u32[]{:S(2)}) async-start(bf16[1,8,64,288]{3,2,0,1:T(8,128)(2,1)} %bitcast.5), calls=%async_computation.1 | async-start | bytes 786432 | tf_op jit(solution)/shard_map/all_to_all | solution.py:93
  43.8 0.4 reshape_squeeze.11
  44.2 0.8 copy.63
  45.0 20.7 %all-to-all-done.1 = bf16[1,8,64,288]{3,2,0,1:T(8,128)(2,1)S(1)} async-done(((bf16[1,8,64,288]{3,2,0,1:T(8,128)(2,1)}), bf16[1,8,64,288]{3,2,0,1:T(8,128)(2,1)S(1)}, u32[]{:S(2)}, u32[]{:S(2)}) %all-to-all-start.1) | async-done | bytes 294944 | tf_op jit(solution)/shard_map/all_to_all | solution.py:93
  65.7 3.5 %all-to-all-start.3 = ((bf16[1,8,64,288]{3,2,0,1:T(8,128)(2,1)}), bf16[1,8,64,288]{3,2,0,1:T(8,128)(2,1)S(1)}, u32[]{:S(2)}, u32[]{:S(2)}) async-start(bf16[1,8,64,288]{3,2,0,1:T(8,128)(2,1)} %bitcast.12), calls=%async_computation.3 | async-start | bytes 786432 | tf_op jit(solution)/shard_map/all_to_all | solution.py:93
  69.2 20.1 %all-gather.2.cloned.1.call-done = bf16[1152,1152]{1,0:T(8,128)(2,1)} async-done(((bf16[288,1152]{1,0:T(8,128)(2,1)}), bf16[1152,1152]{1,0:T(8,128)(2,1)}) %all-gather.2.cloned.1.call-update) | async-done | bytes 2654224 | tf_op jit(solution)/shard_map/all_gather | solution.py:84
  89.3 2.7 %convolution_convert_fusion = bf16[128,1152]{1,0:T(8,128)(2,1)S(1)} fusion(bf16[1152,1152]{1,0:T(8,128)(2,1)} %all-gather.2.cloned.1.call-done, bf16[1,128,1152]{2,1,0:T(8,128)(2,1)S(1)} %copy-done.1, f32[1152]{0:T(1024)S(1)} %copy-done.5), kind=kOutput, calls=%fused_computation.2 | convolution fusion | flops 340328448 | bytes 3248640 | tf_op jit(solution)/shard_map/dot_general | solution.py:82
  91.9 0.4 reshape.84
  92.3 0.8 copy.61
  93.1 3.5 %all-to-all-start.2 = ((bf16[1,8,64,288]{3,2,0,1:T(8,128)(2,1)}), bf16[1,8,64,288]{3,2,0,1:T(8,128)(2,1)S(1)}, u32[]{:S(2)}, u32[]{:S(2)}) async-start(bf16[1,8,64,288]{3,2,0,1:T(8,128)(2,1)} %bitcast.9), calls=%async_computation.2 | async-start | bytes 786432 | tf_op jit(solution)/shard_map/all_to_all | solution.py:93
  96.6 0.3 reshape_reshape.24
  97.0 0.3 reshape_reshape.25
  97.3 1.1 reshape_reshape.27
  98.4 2.1 %fusion.36 = (f32[64,4,8]{2,1,0:T(4,128)S(1)}, f32[64,4,8,8]{2,3,1,0:T(8,128)}) fusion(bf16[8,64,4,72]{3,2,1,0:T(4,128)(2,1)S(1)} %reshape_reshape.25, bf16[8,64,4,72]{3,2,1,0:T(4,128)(2,1)S(1)} %reshape_reshape.24), kind=kOutput, calls=%fused_computation.37 | convolution fusion | flops 2408455 | bytes 663552 | tf_op jit(solution)/shard_map/sub | solution.py:30
  100.5 8.1 %all-to-all-done.2 = bf16[1,8,64,288]{3,2,0,1:T(8,128)(2,1)S(1)} async-done(((bf16[1,8,64,288]{3,2,0,1:T(8,128)(2,1)}), bf16[1,8,64,288]{3,2,0,1:T(8,128)(2,1)S(1)}, u32[]{:S(2)}, u32[]{:S(2)}) %all-to-all-start.2) | async-done | bytes 294944 | tf_op jit(solution)/shard_map/all_to_all | solution.py:93
  108.6 0.3 reshape_reshape.26
  109.0 3.1 %multiply_reduce_fusion = (f32[8,64,4]{0,2,1:T(4,128)S(1)}, bf16[8,64,4,72]{3,0,2,1:T(8,128)(2,1)}) fusion(bf16[8,64,4,72]{3,2,1,0:T(4,128)(2,1)S(1)} %reshape_reshape.26, bf16[8,64,4,72]{3,2,1,0:T(4,128)(2,1)} %reshape_reshape.27, f32[64,4,8,8]{2,3,1,0:T(8,128)} %get-tuple-element.5, f32[64,4,8]{2,1,0:T(4,128)S(1)} %get-tuple-element.4), kind=kOutput, calls=%fused_computation.19 | convolution fusion | flops 3127296 | bytes 966656 | tf_op jit(solution)/shard_map/phfg,gphd->fphd/dot_general | solution.py:33
  112.1 0.8 fusion.5
  112.9 0.5 fusion.8
  113.6 1.1 reshape_reshape.29
  114.7 3.6 %all-to-all-start.5 = ((bf16[8,1,64,288]{3,2,1,0:T(8,128)(2,1)}), bf16[8,1,64,288]{3,2,1,0:T(8,128)(2,1)S(1)}, u32[]{:S(2)}, u32[]{:S(2)}) async-start(bf16[8,1,64,288]{3,2,1,0:T(8,128)(2,1)} %bitcast.20), calls=%async_computation.5 | async-start | bytes 786432 | tf_op jit(solution)/shard_map/all_to_all | solution.py:101
  118.3 0.5 fusion.7
  119.1 1.1 reshape_reshape.28
  120.2 10.0 %all-to-all-done.5 = bf16[8,1,64,288]{3,2,1,0:T(8,128)(2,1)S(1)} async-done(((bf16[8,1,64,288]{3,2,1,0:T(8,128)(2,1)}), bf16[8,1,64,288]{3,2,1,0:T(8,128)(2,1)S(1)}, u32[]{:S(2)}, u32[]{:S(2)}) %all-to-all-start.5) | async-done | bytes 294944 | tf_op jit(solution)/shard_map/all_to_all | solution.py:101
  130.2 3.6 %all-to-all-start.4 = ((bf16[8,1,64,288]{3,2,1,0:T(8,128)(2,1)}), bf16[8,1,64,288]{3,2,1,0:T(8,128)(2,1)S(1)}, u32[]{:S(2)}, u32[]{:S(2)}) async-start(bf16[8,1,64,288]{3,2,1,0:T(8,128)(2,1)} %bitcast.16), calls=%async_computation.4 | async-start | bytes 786432 | tf_op jit(solution)/shard_map/all_to_all | solution.py:101
  133.8 1.2 copy.84
  135.1 1.1 reshape_reshape.31
  136.2 9.4 %all-to-all-done.4 = bf16[8,1,64,288]{3,2,1,0:T(8,128)(2,1)S(1)} async-done(((bf16[8,1,64,288]{3,2,1,0:T(8,128)(2,1)}), bf16[8,1,64,288]{3,2,1,0:T(8,128)(2,1)S(1)}, u32[]{:S(2)}, u32[]{:S(2)}) %all-to-all-start.4) | async-done | bytes 294944 | tf_op jit(solution)/shard_map/all_to_all | solution.py:101
  145.6 4.1 %all-to-all-start.7 = ((bf16[8,1,64,288]{3,2,1,0:T(8,128)(2,1)}), bf16[8,1,64,288]{3,2,1,0:T(8,128)(2,1)}, u32[]{:S(2)}, u32[]{:S(2)}) async-start(bf16[8,1,64,288]{3,2,1,0:T(8,128)(2,1)} %bitcast.28), calls=%async_computation.7 | async-start | bytes 786432 | tf_op jit(solution)/shard_map/all_to_all | solution.py:101
  149.7 1.8 fusion.9
  151.7 1.1 reshape_reshape.30
  152.8 8.3 %all-to-all-done.7 = bf16[8,1,64,288]{3,2,1,0:T(8,128)(2,1)} async-done(((bf16[8,1,64,288]{3,2,1,0:T(8,128)(2,1)}), bf16[8,1,64,288]{3,2,1,0:T(8,128)(2,1)}, u32[]{:S(2)}, u32[]{:S(2)}) %all-to-all-start.7) | async-done | bytes 294944 | tf_op jit(solution)/shard_map/all_to_all | solution.py:101
  161.1 4.3 %all-to-all-start.6 = ((bf16[8,1,64,288]{3,2,1,0:T(8,128)(2,1)}), bf16[8,1,64,288]{3,2,1,0:T(8,128)(2,1)}, u32[]{:S(2)}, u32[]{:S(2)}) async-start(bf16[8,1,64,288]{3,2,1,0:T(8,128)(2,1)} %bitcast.73), calls=%async_computation.6 | async-start | bytes 786432 | tf_op jit(solution)/shard_map/all_to_all | solution.py:101
  165.4 1.1 copy.79
  166.4 2.0 %reshape.90 = bf16[1,128,1152]{2,1,0:T(8,128)(2,1)} reshape(bf16[2,64,4,288]{3,2,1,0:T(4,128)(2,1)} %copy.79) | data formatting | bytes 589824 | tf_op jit(solution)/shard_map/reshape | solution.py:69
  168.8 1.0 reshape.88
  169.8 1.3 copy.122
  171.4 1.6 fusion.10
  172.9 22.4 %psum.7 = f32[1152]{0:T(1024)} all-reduce(f32[1152]{0:T(1024)S(1)} %fusion.10), channel_id=1, replica_groups=mesh['clip'=4,'tx'=4,'ty'=2] {'tx','ty'}, use_global_device_ids=true, to_apply=%region_4.0 | all-reduce | flops 1152 | bytes 9216 | tf_op jit(solution)/shard_map/psum | solution.py:113
  195.4 1.3 copy.83
  196.7 1.0 reshape.92
  (22 shorter events, 1.3 us)
Async XLA Ops:
  7.2 10.3 %copy-start.3 = (bf16[1,128,1152]{2,1,0:T(8,128)(2,1)S(1)}, bf16[1,128,1152]{2,1,0:T(8,128)(2,1)}, u32[]{:S(2)}) copy-start(bf16[1,128,1152]{2,1,0:T(8,128)(2,1)} %param.7) | copy-start | bytes 884740
  7.2 36.7 %copy-start.4 = (bf16[1,128,1152]{2,1,0:T(8,128)(2,1)S(1)}, bf16[1,128,1152]{2,1,0:T(8,128)(2,1)}, u32[]{:S(2)}) copy-start(bf16[1,128,1152]{2,1,0:T(8,128)(2,1)} %param.8) | copy-start | bytes 884740
  7.2 82.1 %all-gather.2.cloned.1.call-start = ((), (), s32[]{:S(2)}) async-start(), calls=%async_computation.8 | async-start | bytes 3317760 | tf_op jit(solution)/shard_map/all_gather | solution.py:84
  10.1 79.2 %copy-start.1 = (bf16[1,128,1152]{2,1,0:T(8,128)(2,1)S(1)}, bf16[1,128,1152]{2,1,0:T(8,128)(2,1)}, u32[]{:S(2)}) copy-start(bf16[1,128,1152]{2,1,0:T(8,128)(2,1)} %param.9) | copy-start | bytes 884740
  10.1 79.2 %copy-start.5 = (f32[1152]{0:T(1024)S(1)}, f32[1152]{0:T(1024)}, u32[]{:S(2)}) copy-start(f32[1152]{0:T(1024)} %param.10) | copy-start | bytes 13828
  10.1 27.7 %all-to-all-start = ((bf16[1,8,64,288]{3,2,0,1:T(8,128)(2,1)}), bf16[1,8,64,288]{3,2,0,1:T(8,128)(2,1)S(1)}, u32[]{:S(2)}, u32[]{:S(2)}) async-start(bf16[1,8,64,288]{3,2,0,1:T(8,128)(2,1)} %bitcast.2), calls=%async_computation | async-start | bytes 786432 | tf_op jit(solution)/shard_map/all_to_all | solution.py:93
  37.8 28.0 %all-to-all-start.1 = ((bf16[1,8,64,288]{3,2,0,1:T(8,128)(2,1)}), bf16[1,8,64,288]{3,2,0,1:T(8,128)(2,1)S(1)}, u32[]{:S(2)}, u32[]{:S(2)}) async-start(bf16[1,8,64,288]{3,2,0,1:T(8,128)(2,1)} %bitcast.5), calls=%async_computation.1 | async-start | bytes 786432 | tf_op jit(solution)/shard_map/all_to_all | solution.py:93
  65.7 27.4 %all-to-all-start.3 = ((bf16[1,8,64,288]{3,2,0,1:T(8,128)(2,1)}), bf16[1,8,64,288]{3,2,0,1:T(8,128)(2,1)S(1)}, u32[]{:S(2)}, u32[]{:S(2)}) async-start(bf16[1,8,64,288]{3,2,0,1:T(8,128)(2,1)} %bitcast.12), calls=%async_computation.3 | async-start | bytes 786432 | tf_op jit(solution)/shard_map/all_to_all | solution.py:93
  93.1 15.5 %all-to-all-start.2 = ((bf16[1,8,64,288]{3,2,0,1:T(8,128)(2,1)}), bf16[1,8,64,288]{3,2,0,1:T(8,128)(2,1)S(1)}, u32[]{:S(2)}, u32[]{:S(2)}) async-start(bf16[1,8,64,288]{3,2,0,1:T(8,128)(2,1)} %bitcast.9), calls=%async_computation.2 | async-start | bytes 786432 | tf_op jit(solution)/shard_map/all_to_all | solution.py:93
  108.9 3.1 %copy-start.2 = (bf16[8,64,4,72]{3,2,1,0:T(4,128)(2,1)S(1)}, bf16[8,64,4,72]{3,2,1,0:T(4,128)(2,1)}, u32[]{:S(2)}) copy-start(bf16[8,64,4,72]{3,2,1,0:T(4,128)(2,1)} %reshape_reshape.27) | copy-start | bytes 884740
  108.9 3.1 %copy-start.6 = (f32[64,4,8,8]{2,3,1,0:T(8,128)S(1)}, f32[64,4,8,8]{2,3,1,0:T(8,128)}, u32[]{:S(2)}) copy-start(f32[64,4,8,8]{2,3,1,0:T(8,128)} %get-tuple-element.5) | copy-start | bytes 196612
  114.7 15.5 %all-to-all-start.5 = ((bf16[8,1,64,288]{3,2,1,0:T(8,128)(2,1)}), bf16[8,1,64,288]{3,2,1,0:T(8,128)(2,1)S(1)}, u32[]{:S(2)}, u32[]{:S(2)}) async-start(bf16[8,1,64,288]{3,2,1,0:T(8,128)(2,1)} %bitcast.20), calls=%async_computation.5 | async-start | bytes 786432 | tf_op jit(solution)/shard_map/all_to_all | solution.py:101
  130.2 15.4 %all-to-all-start.4 = ((bf16[8,1,64,288]{3,2,1,0:T(8,128)(2,1)}), bf16[8,1,64,288]{3,2,1,0:T(8,128)(2,1)S(1)}, u32[]{:S(2)}, u32[]{:S(2)}) async-start(bf16[8,1,64,288]{3,2,1,0:T(8,128)(2,1)} %bitcast.16), calls=%async_computation.4 | async-start | bytes 786432 | tf_op jit(solution)/shard_map/all_to_all | solution.py:101
  145.6 15.5 %all-to-all-start.7 = ((bf16[8,1,64,288]{3,2,1,0:T(8,128)(2,1)}), bf16[8,1,64,288]{3,2,1,0:T(8,128)(2,1)}, u32[]{:S(2)}, u32[]{:S(2)}) async-start(bf16[8,1,64,288]{3,2,1,0:T(8,128)(2,1)} %bitcast.28), calls=%async_computation.7 | async-start | bytes 786432 | tf_op jit(solution)/shard_map/all_to_all | solution.py:101
  152.8 18.6 %copy-start = (bf16[1152,1152]{1,0:T(8,128)(2,1)S(1)}, bf16[1152,1152]{1,0:T(8,128)(2,1)}, u32[]{:S(2)}) copy-start(bf16[1152,1152]{1,0:T(8,128)(2,1)} %all-gather.2.cloned.1.call-done) | copy-start | bytes 7962628
  161.1 34.3 %all-to-all-start.6 = ((bf16[8,1,64,288]{3,2,1,0:T(8,128)(2,1)}), bf16[8,1,64,288]{3,2,1,0:T(8,128)(2,1)}, u32[]{:S(2)}, u32[]{:S(2)}) async-start(bf16[8,1,64,288]{3,2,1,0:T(8,128)(2,1)} %bitcast.73), calls=%async_computation.6 | async-start | bytes 786432 | tf_op jit(solution)/shard_map/all_to_all | solution.py:101
Sparse Core Ops, SparseCore 0:
  9.6 79.6 all-gather.1
where the time goes:
time: 206 us; the launch traced here: 205 us
  waiting for transfers between devices  96.3 us (47%)
  starting transfers between devices  36.2 us (18%)
  blocking collectives  22.4 us (11%)
  local copies, waits for them, and re-layouts  22.3 us (11%)
  between operations  14.2 us (7%)
  matrix products  13 us (6%)
    all_to_all x4, waiting for transfers between devices, per_device(): lax.all_to_all(shortened(prepared), ('tx', 'ty'), split_axis=1, concat_ax...  47.9 us
    all_to_all x4, waiting for transfers between devices, per_device(): lax.all_to_all(shortened(outgoing), ('tx', 'ty'), split_axis=0, concat_ax...  27.7 us
    psum x1, blocking collectives, per_device(): gate_grad = lax.psum(local_terms, ('tx', 'ty'))  22.4 us
    all_to_all x4, starting transfers between devices, per_device(): lax.all_to_all(shortened(prepared), ('tx', 'ty'), split_axis=1, concat_ax...  20.5 us
    all_gather x1, waiting for transfers between devices, per_device(): lax.all_gather(out_weight, 'tx', axis=0, tiled=True)  20.1 us
    all_to_all x4, starting transfers between devices, per_device(): lax.all_to_all(shortened(outgoing), ('tx', 'ty'), split_axis=0, concat_ax...  15.6 us
    another operation x4, local copies, waits for them, and re-layouts, per_device(): arr.reshape(devices_here, 1, block_pos, block_width)  4.46 us
  transfers between devices with their start and end apart: 9, of which 7 were waited for; matrix products, arithmetic and copies ran while one was open for 13% of the time, Pallas kernels for 0%

commit v1 on v0

--- a/solution.py
+++ b/solution.py
@@ -1,6 +1,10 @@
+import functools
+
 import jax
 import jax.numpy as jnp
 from jax import lax
+from jax.experimental import pallas as pl
+from jax.experimental.pallas import tpu as pltpu
 from jax.sharding import PartitionSpec as P
 
 HEAD_DIM = 72
@@ -69,7 +73,7 @@
     return pieces.reshape(1, across_y * block_pos, across_x * block_width)
 
 
-def per_device(query_states, key_states, value_states, grad_output, branch_gate, out_weight):
+def per_device_plain(query_states, key_states, value_states, grad_output, branch_gate, out_weight):
     across_x = lax.axis_size("tx")
     across_y = lax.axis_size("ty")
     devices_here = across_x * across_y
@@ -114,6 +118,272 @@
     return (query_grad, key_grad, value_grad, gate_grad)
 
 
+LANES = 128
+MESH = pl.DeviceIdType.MESH
+NT = (((1,), (1,)), ((), ()))
+TN = (((0,), (0,)), ((), ()))
+
+
+def dot(a, b, dims=(((1,), (0,)), ((), ()))):
+    return lax.dot_general(a, b, dims, preferred_element_type=jnp.float32)
+
+
+def pack(rows, across_x, block_width, group):
+    full = block_width // LANES
+    rest = block_width % LANES
+    groups = LANES // rest
+    block_pos = group * groups
+    blocks = []
+    for t in range(across_x):
+        base = t * block_width
+        tiles = [rows[:, base + j * LANES : base + (j + 1) * LANES] for j in range(full)]
+        narrow = rows[:, base + full * LANES : base + block_width]
+        for u in range(rows.shape[0] // block_pos):
+            start = u * block_pos
+            parts = [tile[start : start + block_pos] for tile in tiles]
+            parts.append(
+                jnp.concatenate(
+                    [narrow[start + g * group : start + (g + 1) * group] for g in range(groups)], axis=1
+                )
+            )
+            blocks.append((t, u, parts))
+    return blocks
+
+
+def fused_kernel(
+    across_x, across_y, block_width, group,
+    q_ref, k_ref, v_ref, g_ref, gate_ref, w_ref,
+    dq_ref, dk_ref, dv_ref, gg_ref,
+    send_pack, recv_pack, recv_g, out_pack, ret_pack, w_aug, gate_own, gate_all,
+    fs, fr, gs, gr, rs, rr, ps, pr,
+):
+    n = across_x * across_y
+    mx, my = lax.axis_index("tx"), lax.axis_index("ty")
+    me = mx * across_y + my
+    full = block_width // LANES
+    rest = block_width % LANES
+    groups = LANES // rest
+    block_pos = group * groups
+    tiles = full + 1
+    rows = n * group
+    heads = block_width // HEAD_DIM
+    factor = HEAD_DIM ** (-0.5)
+
+    def ident(d):
+        return {"tx": d // across_y, "ty": d % across_y}
+
+    def other(o):
+        return lax.rem(me + o, n)
+
+    barrier = pltpu.get_barrier_semaphore()
+    for o in range(1, n):
+        pl.semaphore_signal(barrier, inc=1, device_id=ident(other(o)), device_id_type=MESH)
+    pl.semaphore_wait(barrier, n - 1)
+
+    def remote(src, dst, ss, sr, d):
+        return pltpu.make_async_remote_copy(
+            src_ref=src, dst_ref=dst, send_sem=ss, recv_sem=sr, device_id=ident(d), device_id_type=MESH
+        )
+
+    started = []
+    for o in range(1, n):
+        d = other(o)
+        copy = remote(g_ref.at[d % across_y], recv_g.at[me], gs.at[d], gr.at[me], d)
+        copy.start()
+        started.append(copy)
+    for a, ref in enumerate((q_ref, k_ref, v_ref)):
+        for t, u, parts in pack(ref[...], across_x, block_width, group):
+            d = t * across_y + u
+            for j, part in enumerate(parts):
+                send_pack[a, d, j * block_pos : j * block_pos + part.shape[0], :] = part
+        for o in range(1, n):
+            d = other(o)
+            copy = remote(send_pack.at[a, d], recv_pack.at[a, me], fs.at[a, d], fr.at[a, me], d)
+            copy.start()
+            started.append(copy)
+        recv_pack[a, me] = send_pack[a, me]
+    recv_g[me] = g_ref[my]
+    w_aug[: full * LANES, :] = w_ref[: full * LANES, :]
+    for g in range(groups):
+        w_aug[full * LANES + g * rest : full * LANES + (g + 1) * rest, :] = w_ref[full * LANES :, :]
+    for a in range(3):
+        out_pack[a, :, full * block_pos :, :] = jnp.zeros((n, group, LANES), jnp.bfloat16)
+    gate_own[...] = jnp.zeros_like(gate_own)
+
+    for o in range(1, n):
+        s = other(o)
+        remote(recv_g.at[s], recv_g.at[s], gs.at[s], gr.at[s], s).wait_recv()
+        for a in range(3):
+            remote(recv_pack.at[a, s], recv_pack.at[a, s], fs.at[a, s], fr.at[a, s], s).wait_recv()
+
+    lane = lax.broadcasted_iota(jnp.int32, (1, tiles * LANES), 1)
+    row_pos = lax.broadcasted_iota(jnp.int32, (rows, rows), 0) % group
+    col_pos = lax.broadcasted_iota(jnp.int32, (rows, rows), 1) % group
+    same = row_pos == col_pos
+
+    def one_group(g, carry):
+        start = pl.multiple_of(g * group, group)
+        tail = lane - full * LANES
+        channel = jnp.where(
+            tail < 0, lane, jnp.where(tail // rest == g, full * LANES + tail % rest, block_width)
+        )
+        head_of = channel // HEAD_DIM
+
+        def load(a):
+            parts = []
+            for j in range(full):
+                at = pl.multiple_of(j * block_pos + start, group)
+                parts.append(recv_pack[a, :, pl.ds(at, group), :].reshape(rows, LANES))
+            parts.append(recv_pack[a, :, full * block_pos :, :].reshape(rows, LANES))
+            return parts
+
+        qt, kt, vt = load(0), load(1), load(2)
+        grads = recv_g[:, pl.ds(start, group), :].reshape(rows, recv_g.shape[2]).astype(jnp.float32)
+        gated = (grads * gate_ref[...]).astype(jnp.bfloat16)
+        d_attn = dot(gated, w_aug[...], NT).astype(jnp.bfloat16)
+        gt = [d_attn[:, j * LANES : (j + 1) * LANES] for j in range(tiles)]
+        results = [[jnp.zeros((rows, LANES), jnp.float32) for _ in range(tiles)] for _ in range(4)]
+        for h in range(heads):
+            first = h * HEAD_DIM // LANES
+            last = (h * HEAD_DIM + HEAD_DIM - 1) // LANES
+            span = range(first, last + 1)
+            mask = head_of[:, first * LANES : (last + 1) * LANES] == h
+            ones = jnp.where(mask, 1.0, 0.0)
+            keep = ones.astype(jnp.bfloat16)
+
+            def window(parts):
+                return jnp.concatenate([parts[j] for j in span], axis=1)
+
+            qw, kw, vw, gw = window(qt), window(kt), window(vt), window(gt)
+            gm = gw * keep
+            scores = dot(qw * keep, kw, NT) * factor
+            scores = jnp.where(same, scores, -1e30)
+            peak = jnp.max(scores, axis=-1, keepdims=True)
+            expon = jnp.exp(scores - peak)
+            probs = expon / jnp.sum(expon, axis=-1, keepdims=True)
+            probs_b = probs.astype(jnp.bfloat16)
+            out_w = dot(probs_b, vw)
+            dv_w = dot(probs_b, gw, TN)
+            dprobs = dot(gm, vw, NT)
+            out_b = out_w.astype(jnp.bfloat16).astype(jnp.float32)
+            delta = jnp.sum(gm.astype(jnp.float32) * out_b, axis=-1, keepdims=True)
+            dscores = (probs * (dprobs - delta) * factor).astype(jnp.bfloat16)
+            dq_w = dot(dscores, kw)
+            dk_w = dot(dscores, qw, TN)
+            for which, value in enumerate((dq_w, dk_w, dv_w, out_w)):
+                for i, j in enumerate(span):
+                    at = slice(i * LANES, (i + 1) * LANES)
+                    results[which][j] = jnp.where(mask[:, at], value[:, at], results[which][j])
+        for which in range(3):
+            for j in range(full):
+                at = pl.multiple_of(j * block_pos + start, group)
+                out_pack[which, :, pl.ds(at, group), :] = (
+                    results[which][j].astype(jnp.bfloat16).reshape(n, group, LANES)
+                )
+            old = out_pack[which, :, full * block_pos :, :].reshape(rows, LANES).astype(jnp.float32)
+            out_pack[which, :, full * block_pos :, :] = (
+                (old + results[which][full]).astype(jnp.bfloat16).reshape(n, group, LANES)
+            )
+        attn = jnp.concatenate(results[3], axis=1).astype(jnp.bfloat16)
+        branch = dot(attn, w_aug[...])
+        gate_own[...] += jnp.sum(grads * branch, axis=0, keepdims=True)
+        return carry
+
+    lax.fori_loop(0, groups, one_group, 0)
+
+    for o in range(1, n):
+        d = other(o)
+        copy = remote(gate_own, gate_all.at[me], ps.at[d], pr.at[me], d)
+        copy.start()
+        started.append(copy)
+        for a in range(3):
+            copy = remote(out_pack.at[a, d], ret_pack.at[a, me], rs.at[a, d], rr.at[a, me], d)
+            copy.start()
+            started.append(copy)
+    for a in range(3):
+        ret_pack[a, me] = out_pack[a, me]
+    gate_all[me] = gate_own[...]
+
+    for o in range(1, n):
+        s = other(o)
+        remote(gate_own, gate_all.at[s], ps.at[s], pr.at[s], s).wait_recv()
+    total = gate_all[0]
+    for s in range(1, n):
+        total += gate_all[s]
+    gg_ref[...] = total
+    for a, ref in enumerate((dq_ref, dk_ref, dv_ref)):
+        for o in range(1, n):
+            s = other(o)
+            remote(ret_pack.at[a, s], ret_pack.at[a, s], rs.at[a, s], rr.at[a, s], s).wait_recv()
+        for u in range(across_y):
+            pieces = []
+            for t in range(across_x):
+                d = t * across_y + u
+                for j in range(full):
+                    pieces.append(ret_pack[a, d, j * block_pos : (j + 1) * block_pos, :])
+                narrow = ret_pack[a, d, full * block_pos :, :]
+                pieces.append(
+                    jnp.concatenate([narrow[:, g * rest : (g + 1) * rest] for g in range(groups)], axis=0)
+                )
+            ref[u * block_pos : (u + 1) * block_pos, :] = jnp.concatenate(pieces, axis=1)
+    for copy in started:
+        copy.wait_send()
+
+
+def per_device(query_states, key_states, value_states, grad_output, branch_gate, out_weight):
+    across_x = lax.axis_size("tx")
+    across_y = lax.axis_size("ty")
+    n = across_x * across_y
+    frames_here, positions, width = grad_output.shape
+    block_pos = positions // across_y
+    block_width = width // across_x
+    rest = block_width % LANES
+    fits = (
+        frames_here == 1
+        and rest > 0
+        and LANES % rest == 0
+        and rest % 16 == 0
+        and block_width % HEAD_DIM == 0
+        and block_pos % (LANES // rest * 16) == 0
+        and n * block_pos * rest // LANES <= 2 * LANES
+        and width % LANES == 0
+    )
+    if not fits:
+        return per_device_plain(
+            query_states, key_states, value_states, grad_output, branch_gate, out_weight
+        )
+    group = block_pos * rest // LANES
+    packed = block_pos * block_width // LANES
+    bf16, f32 = jnp.bfloat16, jnp.float32
+    dma = pltpu.SemaphoreType.DMA
+    grads = jax.ShapeDtypeStruct((positions, width), bf16)
+    vmem = pl.BlockSpec(memory_space=pltpu.VMEM)
+    dq, dk, dv, gate = pl.pallas_call(
+        functools.partial(fused_kernel, across_x, across_y, block_width, group),
+        out_shape=(grads, grads, grads, jax.ShapeDtypeStruct((1, width), f32)),
+        in_specs=[vmem] * 6,
+        out_specs=(vmem,) * 4,
+        scratch_shapes=[
+            pltpu.VMEM((3, n, packed, LANES), bf16),
+            pltpu.VMEM((3, n, packed, LANES), bf16),
+            pltpu.VMEM((n, block_pos, width), bf16),
+            pltpu.VMEM((3, n, packed, LANES), bf16),
+            pltpu.VMEM((3, n, packed, LANES), bf16),
+            pltpu.VMEM(((block_width // LANES + 1) * LANES, width), bf16),
+            pltpu.VMEM((1, width), f32),
+            pltpu.VMEM((n, 1, width), f32),
+            dma((3, n)), dma((3, n)), dma((n,)), dma((n,)),
+            dma((3, n)), dma((3, n)), dma((n,)), dma((n,)),
+        ],
+        compiler_params=pltpu.CompilerParams(collective_id=0, has_side_effects=True),
+    )(
+        query_states[0], key_states[0], value_states[0],
+        grad_output.reshape(across_y, block_pos, width),
+        branch_gate.reshape(1, width), out_weight,
+    )
+    return dq[None], dk[None], dv[None], gate.reshape(width)
+
+
 def solution(mesh):
     in_specs = (
         P(("clip", "tx", "ty"), None, None),

time: 206 us -> 90.1 us (0.44)
  the two profiles are of different devices: /device:TPU:0 before, /device:TPU:28 now
where the time goes in v1:
time: 90.1 us; the launch traced here: 89.8 us
  Pallas kernels  83 us (92%)
  local copies, waits for them, and re-layouts  5.5 us (6%)
    pallas_call x1, Pallas kernels, per_device(): pl.pallas_call(functools.partial(fused_kernel, across_x, across_y, block_...  83 us
    unnamed x9, local copies, waits for them, and re-layouts  4.21 us

profile of v1, /device:TPU:28, one launch (start us, length us, event | category | flops | bytes accessed | tf_op | source)
XLA Modules:
  0.0 89.8 jit_solution(5356771298923671512)
XLA Ops:
  0.6 1.3 %reshape.18.gate_ref = f32[1,1152]{1,0:T(1,128)} reshape(f32[1152]{0:T(1024)} %param.10) | data formatting | bytes 9216 | tf_op jit(solution)/shard_map/reshape | solution.py:382
  1.9 83.0 %shard_map.93 = (bf16[128,1152]{1,0:T(8,128)(2,1)}, bf16[128,1152]{1,0:T(8,128)(2,1)}, bf16[128,1152]{1,0:T(8,128)(2,1)}, f32[1,1152]{1,0:T(1,128)}) custom-call(bf16[128,1152]{1,0:T(8,128)(2,1)} %bitcast.10, bf16[128,1152]{1,0:T(8,128)(2,1)} %bitcast.11, bf16[128,1152]{1,0:T(8,128)(2,1)} %bitcast.12, bf16[2,64,1152]{2,1,0:T(8,128)(2,1)} %bitcast.13, ...), custom_call_target="tpu_custom_call" | custom-call | tf_op jit(solution)/shard_map/pallas_call | solution.py:361
  84.9 0.0 copy-start.2
  84.9 0.7 copy-done.2
  85.6 0.6 reduce
  86.2 0.0 copy-start.1
  86.2 1.7 %copy.13 = bf16[1,128,1152]{2,1,0:T(8,128)(2,1)} copy(bf16[1,128,1152]{2,1,0:T(8,128)(2,1)} %bitcast.9) | data formatting | bytes 589824
  88.0 0.0 copy-done.1
  88.0 0.0 copy-start
  88.0 0.7 copy.14
  88.7 0.4 copy-done
  89.1 0.7 copy.15
Async XLA Ops:
  84.9 0.7 copy-start.2
  86.2 1.7 %copy-start.1 = (bf16[128,1152]{1,0:T(8,128)(2,1)S(1)}, bf16[128,1152]{1,0:T(8,128)(2,1)}, u32[]{:S(2)}) copy-start(bf16[128,1152]{1,0:T(8,128)(2,1)} %get-tuple-element.9) | copy-start | bytes 884740
  88.0 1.1 %copy-start = (bf16[128,1152]{1,0:T(8,128)(2,1)S(1)}, bf16[128,1152]{1,0:T(8,128)(2,1)}, u32[]{:S(2)}) copy-start(bf16[128,1152]{1,0:T(8,128)(2,1)} %get-tuple-element.10) | copy-start | bytes 884740

commit v2 on v1

--- a/solution.py
+++ b/solution.py
@@ -119,6 +119,7 @@
 
 
 LANES = 128
+CHUNKS = 2
 MESH = pl.DeviceIdType.MESH
 NT = (((1,), (1,)), ((), ()))
 TN = (((0,), (0,)), ((), ()))
@@ -154,8 +155,8 @@
     across_x, across_y, block_width, group,
     q_ref, k_ref, v_ref, g_ref, gate_ref, w_ref,
     dq_ref, dk_ref, dv_ref, gg_ref,
-    send_pack, recv_pack, recv_g, out_pack, ret_pack, w_aug, gate_own, gate_all,
-    fs, fr, gs, gr, rs, rr, ps, pr,
+    send0, send1, recv0, recv1, recv_g, out0, out1, ret0, ret1, w_aug, gate_own, gate_all,
+    gs, gr, ws, s0s, s0r, s1s, s1r, r0s, r0r, r1s, r1r, ps, pr,
 ):
     n = across_x * across_y
     mx, my = lax.axis_index("tx"), lax.axis_index("ty")
@@ -163,66 +164,130 @@
     full = block_width // LANES
     rest = block_width % LANES
     groups = LANES // rest
-    block_pos = group * groups
+    per_chunk = groups // CHUNKS
+    part_pos = group * per_chunk
+    body = full * part_pos
     tiles = full + 1
     rows = n * group
     heads = block_width // HEAD_DIM
     factor = HEAD_DIM ** (-0.5)
+    sends, recvs = (send0, send1), (recv0, recv1)
 
     def ident(d):
         return {"tx": d // across_y, "ty": d % across_y}
 
     def other(o):
         return lax.rem(me + o, n)
+
+    def remote(src, dst, ss, sr, d):
+        return pltpu.make_async_remote_copy(
+            src_ref=src, dst_ref=dst, send_sem=ss, recv_sem=sr, device_id=ident(d), device_id_type=MESH
+        )
 
     barrier = pltpu.get_barrier_semaphore()
     for o in range(1, n):
         pl.semaphore_signal(barrier, inc=1, device_id=ident(other(o)), device_id_type=MESH)
     pl.semaphore_wait(barrier, n - 1)
 
-    def remote(src, dst, ss, sr, d):
-        return pltpu.make_async_remote_copy(
-            src_ref=src, dst_ref=dst, send_sem=ss, recv_sem=sr, device_id=ident(d), device_id_type=MESH
-        )
-
-    started = []
-    for o in range(1, n):
-        d = other(o)
-        copy = remote(g_ref.at[d % across_y], recv_g.at[me], gs.at[d], gr.at[me], d)
-        copy.start()
-        started.append(copy)
+    def span_of(c):
+        return pl.ds(c * part_pos, part_pos)
+
+    def own_grads(act):
+        for c in range(CHUNKS):
+            for i, step in enumerate((1, -1, 0)):
+                for v in range(across_y):
+                    u = lax.rem(my + v, across_y)
+                    to = mx + step
+                    if step == 0 and v == 0:
+                        continue
+
+                    @pl.when((to >= 0) & (to < across_x))
+                    def _():
+                        act(
+                            remote(
+                                g_ref.at[u, span_of(c)], recv_g.at[me, span_of(c)],
+                                gs.at[c, i * across_y + v], gr.at[c, me], to * across_y + u,
+                            )
+                        )
+
+    def frame_wait(f, c):
+        here = recv_g.at[f, span_of(c)]
+        remote(here, here, ws.at[c, f], gr.at[c, f], lax.rem(me + 1, n)).wait_recv()
+
+    def moving(f, c, step):
+        here = recv_g.at[f, span_of(c)]
+        return remote(here, here, ws.at[c, f], gr.at[c, f], me + step * across_y)
+
+    def relays(act):
+        for s in range(1, across_x - 1):
+            for c in range(CHUNKS):
+                for step in (1, -1):
+                    origin = mx - s * step
+                    last = across_x - 1 if step == 1 else 0
+
+                    @pl.when((origin >= 0) & (origin < across_x) & (mx != last))
+                    def _():
+                        for u in range(across_y):
+                            act(origin * across_y + u, c, step)
+
+    def relay(f, c, step):
+        frame_wait(f, c)
+        moving(f, c, step).start()
+
+    own_grads(lambda copy: copy.start())
     for a, ref in enumerate((q_ref, k_ref, v_ref)):
         for t, u, parts in pack(ref[...], across_x, block_width, group):
             d = t * across_y + u
-            for j, part in enumerate(parts):
-                send_pack[a, d, j * block_pos : j * block_pos + part.shape[0], :] = part
+            for c in range(CHUNKS):
+                for j in range(full):
+                    sends[c][d, a, j * part_pos : (j + 1) * part_pos, :] = parts[j][
+                        c * part_pos : (c + 1) * part_pos
+                    ]
+            send0[d, a, body:, :] = parts[full]
+    relays(relay)
+
+    started = []
+    for c, (ss, sr) in enumerate(((s0s, s0r), (s1s, s1r))):
         for o in range(1, n):
             d = other(o)
-            copy = remote(send_pack.at[a, d], recv_pack.at[a, me], fs.at[a, d], fr.at[a, me], d)
+            copy = remote(sends[c].at[d], recvs[c].at[me], ss.at[d], sr.at[me], d)
             copy.start()
             started.append(copy)
-        recv_pack[a, me] = send_pack[a, me]
+        recvs[c][me] = sends[c][me]
     recv_g[me] = g_ref[my]
     w_aug[: full * LANES, :] = w_ref[: full * LANES, :]
     for g in range(groups):
         w_aug[full * LANES + g * rest : full * LANES + (g + 1) * rest, :] = w_ref[full * LANES :, :]
-    for a in range(3):
-        out_pack[a, :, full * block_pos :, :] = jnp.zeros((n, group, LANES), jnp.bfloat16)
+    out1[:, :, body:, :] = jnp.zeros((3, n, group, LANES), jnp.bfloat16)
     gate_own[...] = jnp.zeros_like(gate_own)
 
-    for o in range(1, n):
-        s = other(o)
-        remote(recv_g.at[s], recv_g.at[s], gs.at[s], gr.at[s], s).wait_recv()
-        for a in range(3):
-            remote(recv_pack.at[a, s], recv_pack.at[a, s], fs.at[a, s], fr.at[a, s], s).wait_recv()
+    def arrive(c):
+        for v in range(1, across_y):
+            frame_wait(mx * across_y + lax.rem(my + v, across_y), c)
+        for s in range(1, across_x):
+            for step in (1, -1):
+                origin = mx - s * step
+                last = across_x - 1 if step == 1 else 0
+                early = (mx != last) if s < across_x - 1 else (mx != mx)
+
+                @pl.when((origin >= 0) & (origin < across_x) & jnp.logical_not(early))
+                def _():
+                    for u in range(across_y):
+                        frame_wait(origin * across_y + u, c)
+        ss, sr = ((s0s, s0r), (s1s, s1r))[c]
+        for o in range(1, n):
+            s = other(o)
+            remote(recvs[c].at[s], recvs[c].at[s], ss.at[s], sr.at[s], s).wait_recv()
 
     lane = lax.broadcasted_iota(jnp.int32, (1, tiles * LANES), 1)
     row_pos = lax.broadcasted_iota(jnp.int32, (rows, rows), 0) % group
     col_pos = lax.broadcasted_iota(jnp.int32, (rows, rows), 1) % group
     same = row_pos == col_pos
 
-    def one_group(g, carry):
+    def one_group(c, i, carry):
+        g = c * per_chunk + i
         start = pl.multiple_of(g * group, group)
+        inner = pl.multiple_of(i * group, group)
         tail = lane - full * LANES
         channel = jnp.where(
             tail < 0, lane, jnp.where(tail // rest == g, full * LANES + tail % rest, block_width)
@@ -232,9 +297,9 @@
         def load(a):
             parts = []
             for j in range(full):
-                at = pl.multiple_of(j * block_pos + start, group)
-                parts.append(recv_pack[a, :, pl.ds(at, group), :].reshape(rows, LANES))
-            parts.append(recv_pack[a, :, full * block_pos :, :].reshape(rows, LANES))
+                at = pl.multiple_of(j * part_pos + inner, group)
+                parts.append(recvs[c][:, a, pl.ds(at, group), :].reshape(rows, LANES))
+            parts.append(recv0[:, a, body:, :].reshape(rows, LANES))
             return parts
 
         qt, kt, vt = load(0), load(1), load(2)
@@ -276,12 +341,14 @@
                     results[which][j] = jnp.where(mask[:, at], value[:, at], results[which][j])
         for which in range(3):
             for j in range(full):
-                at = pl.multiple_of(j * block_pos + start, group)
-                out_pack[which, :, pl.ds(at, group), :] = (
-                    results[which][j].astype(jnp.bfloat16).reshape(n, group, LANES)
-                )
-            old = out_pack[which, :, full * block_pos :, :].reshape(rows, LANES).astype(jnp.float32)
-            out_pack[which, :, full * block_pos :, :] = (
+                at = pl.ds(pl.multiple_of(j * part_pos + inner, group), group)
+                value = results[which][j].astype(jnp.bfloat16).reshape(n, group, LANES)
+                if c == 0:
+                    out0[:, which, at, :] = value
+                else:
+                    out1[which, :, at, :] = value
+            old = out1[which, :, body:, :].reshape(rows, LANES).astype(jnp.float32)
+            out1[which, :, body:, :] = (
                 (old + results[which][full]).astype(jnp.bfloat16).reshape(n, group, LANES)
             )
         attn = jnp.concatenate(results[3], axis=1).astype(jnp.bfloat16)
@@ -289,24 +356,35 @@
         gate_own[...] += jnp.sum(grads * branch, axis=0, keepdims=True)
         return carry
 
-    lax.fori_loop(0, groups, one_group, 0)
-
+    arrive(0)
+    lax.fori_loop(0, per_chunk, functools.partial(one_group, 0), 0)
+    for o in range(1, n):
+        d = other(o)
+        copy = remote(out0.at[d], ret0.at[me], r0s.at[d], r0r.at[me], d)
+        copy.start()
+        started.append(copy)
+    arrive(1)
+    lax.fori_loop(0, per_chunk, functools.partial(one_group, 1), 0)
     for o in range(1, n):
         d = other(o)
         copy = remote(gate_own, gate_all.at[me], ps.at[d], pr.at[me], d)
         copy.start()
         started.append(copy)
-        for a in range(3):
-            copy = remote(out_pack.at[a, d], ret_pack.at[a, me], rs.at[a, d], rr.at[a, me], d)
+    for a in range(3):
+        for o in range(1, n):
+            d = other(o)
+            copy = remote(out1.at[a, d], ret1.at[a, me], r1s.at[a, d], r1r.at[a, me], d)
             copy.start()
             started.append(copy)
+    ret0[me] = out0[me]
     for a in range(3):
-        ret_pack[a, me] = out_pack[a, me]
+        ret1[a, me] = out1[a, me]
     gate_all[me] = gate_own[...]
 
     for o in range(1, n):
         s = other(o)
         remote(gate_own, gate_all.at[s], ps.at[s], pr.at[s], s).wait_recv()
+        remote(ret0.at[s], ret0.at[s], r0s.at[s], r0r.at[s], s).wait_recv()
     total = gate_all[0]
     for s in range(1, n):
         total += gate_all[s]
@@ -314,20 +392,24 @@
     for a, ref in enumerate((dq_ref, dk_ref, dv_ref)):
         for o in range(1, n):
             s = other(o)
-            remote(ret_pack.at[a, s], ret_pack.at[a, s], rs.at[a, s], rr.at[a, s], s).wait_recv()
+            remote(ret1.at[a, s], ret1.at[a, s], r1s.at[a, s], r1r.at[a, s], s).wait_recv()
         for u in range(across_y):
             pieces = []
             for t in range(across_x):
                 d = t * across_y + u
                 for j in range(full):
-                    pieces.append(ret_pack[a, d, j * block_pos : (j + 1) * block_pos, :])
-                narrow = ret_pack[a, d, full * block_pos :, :]
+                    at = slice(j * part_pos, (j + 1) * part_pos)
+                    pieces.append(jnp.concatenate([ret0[d, a, at, :], ret1[a, d, at, :]], axis=0))
+                narrow = ret1[a, d, body:, :]
                 pieces.append(
                     jnp.concatenate([narrow[:, g * rest : (g + 1) * rest] for g in range(groups)], axis=0)
                 )
-            ref[u * block_pos : (u + 1) * block_pos, :] = jnp.concatenate(pieces, axis=1)
+            at = slice(u * part_pos * CHUNKS, (u + 1) * part_pos * CHUNKS)
+            ref[at, :] = jnp.concatenate(pieces, axis=1)
     for copy in started:
         copy.wait_send()
+    own_grads(lambda copy: copy.wait_send())
+    relays(lambda f, c, step: moving(f, c, step).wait_send())
 
 
 def per_device(query_states, key_states, value_states, grad_output, branch_gate, out_weight):
@@ -342,6 +424,7 @@
         frames_here == 1
         and rest > 0
         and LANES % rest == 0
+        and LANES // rest % CHUNKS == 0
         and rest % 16 == 0
         and block_width % HEAD_DIM == 0
         and block_pos % (LANES // rest * 16) == 0
@@ -353,7 +436,7 @@
             query_states, key_states, value_states, grad_output, branch_gate, out_weight
         )
     group = block_pos * rest // LANES
-    packed = block_pos * block_width // LANES
+    body = block_pos // CHUNKS * (block_width // LANES)
     bf16, f32 = jnp.bfloat16, jnp.float32
     dma = pltpu.SemaphoreType.DMA
     grads = jax.ShapeDtypeStruct((positions, width), bf16)
@@ -364,15 +447,20 @@
         in_specs=[vmem] * 6,
         out_specs=(vmem,) * 4,
         scratch_shapes=[
-            pltpu.VMEM((3, n, packed, LANES), bf16),
-            pltpu.VMEM((3, n, packed, LANES), bf16),
+            pltpu.VMEM((n, 3, body + group, LANES), bf16),
+            pltpu.VMEM((n, 3, body, LANES), bf16),
+            pltpu.VMEM((n, 3, body + group, LANES), bf16),
+            pltpu.VMEM((n, 3, body, LANES), bf16),
             pltpu.VMEM((n, block_pos, width), bf16),
-            pltpu.VMEM((3, n, packed, LANES), bf16),
-            pltpu.VMEM((3, n, packed, LANES), bf16),
+            pltpu.VMEM((n, 3, body, LANES), bf16),
+            pltpu.VMEM((3, n, body + group, LANES), bf16),
+            pltpu.VMEM((n, 3, body, LANES), bf16),
+            pltpu.VMEM((3, n, body + group, LANES), bf16),
             pltpu.VMEM(((block_width // LANES + 1) * LANES, width), bf16),
             pltpu.VMEM((1, width), f32),
             pltpu.VMEM((n, 1, width), f32),
-            dma((3, n)), dma((3, n)), dma((n,)), dma((n,)),
+            dma((CHUNKS, 3 * across_y)), dma((CHUNKS, n)), dma((CHUNKS, n)),
+            dma((n,)), dma((n,)), dma((n,)), dma((n,)), dma((n,)), dma((n,)),
             dma((3, n)), dma((3, n)), dma((n,)), dma((n,)),
         ],
         compiler_params=pltpu.CompilerParams(collective_id=0, has_side_effects=True),

time: 90.1 us -> 70.7 us (0.78)
  Pallas kernels: 83 us -> 62.9 us
    pallas_call x1, Pallas kernels: 83 us -> 62.9 us  [per_device(): pl.pallas_call(functools.partial(fused_kernel, across_x, across_y, block_...]
where the time goes in v2:
time: 70.7 us; the launch traced here: 69.7 us
  Pallas kernels  62.9 us (89%)
  local copies, waits for them, and re-layouts  5.5 us (8%)
    pallas_call x1, Pallas kernels, per_device(): pl.pallas_call(functools.partial(fused_kernel, across_x, across_y, block_...  62.9 us
    unnamed x9, local copies, waits for them, and re-layouts  4.21 us

profile of v2, /device:TPU:28, one launch (start us, length us, event | category | flops | bytes accessed | tf_op | source)
XLA Modules:
  0.0 69.7 jit_solution(737270450590450041)
XLA Ops:
  0.6 1.3 %reshape.18.gate_ref = f32[1,1152]{1,0:T(1,128)} reshape(f32[1152]{0:T(1024)} %param.10) | data formatting | bytes 9216 | tf_op jit(solution)/shard_map/reshape | solution.py:470
  1.9 62.9 %shard_map.93 = (bf16[128,1152]{1,0:T(8,128)(2,1)}, bf16[128,1152]{1,0:T(8,128)(2,1)}, bf16[128,1152]{1,0:T(8,128)(2,1)}, f32[1,1152]{1,0:T(1,128)}) custom-call(bf16[128,1152]{1,0:T(8,128)(2,1)} %bitcast.10, bf16[128,1152]{1,0:T(8,128)(2,1)} %bitcast.11, bf16[128,1152]{1,0:T(8,128)(2,1)} %bitcast.12, bf16[2,64,1152]{2,1,0:T(8,128)(2,1)} %bitcast.13, ...), custom_call_target="tpu_custom_call" | custom-call | tf_op jit(solution)/shard_map/pallas_call | solution.py:444
  64.8 0.0 copy-start.2
  64.9 0.7 copy-done.2
  65.5 0.6 reduce
  66.2 0.0 copy-start.1
  66.2 1.7 %copy.13 = bf16[1,128,1152]{2,1,0:T(8,128)(2,1)} copy(bf16[1,128,1152]{2,1,0:T(8,128)(2,1)} %bitcast.9) | data formatting | bytes 589824
  67.9 0.0 copy-done.1
  67.9 0.0 copy-start
  67.9 0.7 %copy.14 = bf16[1,128,1152]{2,1,0:T(8,128)(2,1)} copy(bf16[1,128,1152]{2,1,0:T(8,128)(2,1)S(1)} %bitcast.8) | data formatting | bytes 589824
  68.6 0.4 copy-done
  69.0 0.7 %copy.15 = bf16[1,128,1152]{2,1,0:T(8,128)(2,1)} copy(bf16[1,128,1152]{2,1,0:T(8,128)(2,1)S(1)} %bitcast.7) | data formatting | bytes 589824
Async XLA Ops:
  64.8 0.7 copy-start.2
  66.2 1.7 %copy-start.1 = (bf16[128,1152]{1,0:T(8,128)(2,1)S(1)}, bf16[128,1152]{1,0:T(8,128)(2,1)}, u32[]{:S(2)}) copy-start(bf16[128,1152]{1,0:T(8,128)(2,1)} %get-tuple-element.9) | copy-start | bytes 884740
  67.9 1.1 %copy-start = (bf16[128,1152]{1,0:T(8,128)(2,1)S(1)}, bf16[128,1152]{1,0:T(8,128)(2,1)}, u32[]{:S(2)}) copy-start(bf16[128,1152]{1,0:T(8,128)(2,1)} %get-tuple-element.10) | copy-start | bytes 884740

commit v3 on v2

--- a/solution.py
+++ b/solution.py
@@ -153,10 +153,10 @@
 
 def fused_kernel(
     across_x, across_y, block_width, group,
-    q_ref, k_ref, v_ref, g_ref, gate_ref, w_ref,
+    q_hbm, k_hbm, v_hbm, g_hbm, gate_ref, w_hbm,
     dq_ref, dk_ref, dv_ref, gg_ref,
-    send0, send1, recv0, recv1, recv_g, out0, out1, ret0, ret1, w_aug, gate_own, gate_all,
-    gs, gr, ws, s0s, s0r, s1s, s1r, r0s, r0r, r1s, r1r, ps, pr,
+    q_ref, k_ref, v_ref, g_ref, w_ref, done_ref, send0, send1, recv0, recv1, recv_g, out0, out1, ret0, ret1, w_aug, gate_own, gate_all,
+    load_sem, store_sem, gs, gr, ws, s0s, s0r, s1s, s1r, r0s, r0r, r1s, r1r, ps, pr,
 ):
     n = across_x * across_y
     mx, my = lax.axis_index("tx"), lax.axis_index("ty")
@@ -184,6 +184,13 @@
             src_ref=src, dst_ref=dst, send_sem=ss, recv_sem=sr, device_id=ident(d), device_id_type=MESH
         )
 
+    loads = []
+    for i, (src, dst) in enumerate(
+        ((g_hbm, g_ref), (q_hbm, q_ref), (k_hbm, k_ref), (v_hbm, v_ref), (w_hbm, w_ref))
+    ):
+        loads.append(pltpu.make_async_copy(src, dst, load_sem.at[i]))
+        loads[-1].start()
+
     barrier = pltpu.get_barrier_semaphore()
     for o in range(1, n):
         pl.semaphore_signal(barrier, inc=1, device_id=ident(other(o)), device_id_type=MESH)
@@ -234,8 +241,10 @@
         frame_wait(f, c)
         moving(f, c, step).start()
 
+    loads[0].wait()
     own_grads(lambda copy: copy.start())
     for a, ref in enumerate((q_ref, k_ref, v_ref)):
+        loads[1 + a].wait()
         for t, u, parts in pack(ref[...], across_x, block_width, group):
             d = t * across_y + u
             for c in range(CHUNKS):
@@ -255,6 +264,7 @@
             started.append(copy)
         recvs[c][me] = sends[c][me]
     recv_g[me] = g_ref[my]
+    loads[4].wait()
     w_aug[: full * LANES, :] = w_ref[: full * LANES, :]
     for g in range(groups):
         w_aug[full * LANES + g * rest : full * LANES + (g + 1) * rest, :] = w_ref[full * LANES :, :]
@@ -304,7 +314,7 @@
 
         qt, kt, vt = load(0), load(1), load(2)
         grads = recv_g[:, pl.ds(start, group), :].reshape(rows, recv_g.shape[2]).astype(jnp.float32)
-        gated = (grads * gate_ref[...]).astype(jnp.bfloat16)
+        gated = (grads * gate_ref[...].reshape(1, gate_ref.shape[0])).astype(jnp.bfloat16)
         d_attn = dot(gated, w_aug[...], NT).astype(jnp.bfloat16)
         gt = [d_attn[:, j * LANES : (j + 1) * LANES] for j in range(tiles)]
         results = [[jnp.zeros((rows, LANES), jnp.float32) for _ in range(tiles)] for _ in range(4)]
@@ -389,6 +399,7 @@
     for s in range(1, n):
         total += gate_all[s]
     gg_ref[...] = total
+    stores = []
     for a, ref in enumerate((dq_ref, dk_ref, dv_ref)):
         for o in range(1, n):
             s = other(o)
@@ -405,11 +416,29 @@
                     jnp.concatenate([narrow[:, g * rest : (g + 1) * rest] for g in range(groups)], axis=0)
                 )
             at = slice(u * part_pos * CHUNKS, (u + 1) * part_pos * CHUNKS)
-            ref[at, :] = jnp.concatenate(pieces, axis=1)
+            done_ref[a, at, :] = jnp.concatenate(pieces, axis=1)
+        stores.append(pltpu.make_async_copy(done_ref.at[a], ref, store_sem.at[a]))
+        stores[-1].start()
+    for copy in stores:
+        copy.wait()
     for copy in started:
         copy.wait_send()
     own_grads(lambda copy: copy.wait_send())
     relays(lambda f, c, step: moving(f, c, step).wait_send())
+
+
+def hand_over(dq_in, dk_in, dv_in, gate_in, dq_out, dk_out, dv_out, gate_out, held, in_sem, out_sem):
+    pairs = ((dq_in, dq_out), (dk_in, dk_out), (dv_in, dv_out))
+    ins = [pltpu.make_async_copy(src, held.at[i], in_sem.at[i]) for i, (src, _) in enumerate(pairs)]
+    outs = [pltpu.make_async_copy(held.at[i], dst.at[0], out_sem.at[i]) for i, (_, dst) in enumerate(pairs)]
+    for copy in ins:
+        copy.start()
+    gate_out[...] = gate_in[...].reshape(gate_out.shape)
+    for i in range(3):
+        ins[i].wait()
+        outs[i].start()
+    for copy in outs:
+        copy.wait()
 
 
 def per_device(query_states, key_states, value_states, grad_output, branch_gate, out_weight):
@@ -441,12 +470,19 @@
     dma = pltpu.SemaphoreType.DMA
     grads = jax.ShapeDtypeStruct((positions, width), bf16)
     vmem = pl.BlockSpec(memory_space=pltpu.VMEM)
+    anywhere = pl.BlockSpec(memory_space=pl.ANY)
     dq, dk, dv, gate = pl.pallas_call(
         functools.partial(fused_kernel, across_x, across_y, block_width, group),
         out_shape=(grads, grads, grads, jax.ShapeDtypeStruct((1, width), f32)),
-        in_specs=[vmem] * 6,
-        out_specs=(vmem,) * 4,
+        in_specs=[anywhere] * 4 + [vmem, anywhere],
+        out_specs=(anywhere,) * 3 + (vmem,),
         scratch_shapes=[
+            pltpu.VMEM((positions, width), bf16),
+            pltpu.VMEM((positions, width), bf16),
+            pltpu.VMEM((positions, width), bf16),
+            pltpu.VMEM((across_y, block_pos, width), bf16),
+            pltpu.VMEM((block_width, width), bf16),
+            pltpu.VMEM((3, positions, width), bf16),
             pltpu.VMEM((n, 3, body + group, LANES), bf16),
             pltpu.VMEM((n, 3, body, LANES), bf16),
             pltpu.VMEM((n, 3, body + group, LANES), bf16),
@@ -459,7 +495,7 @@
             pltpu.VMEM(((block_width // LANES + 1) * LANES, width), bf16),
             pltpu.VMEM((1, width), f32),
             pltpu.VMEM((n, 1, width), f32),
-            dma((CHUNKS, 3 * across_y)), dma((CHUNKS, n)), dma((CHUNKS, n)),
+            dma((5,)), dma((3,)), dma((CHUNKS, 3 * across_y)), dma((CHUNKS, n)), dma((CHUNKS, n)),
             dma((n,)), dma((n,)), dma((n,)), dma((n,)), dma((n,)), dma((n,)),
             dma((3, n)), dma((3, n)), dma((n,)), dma((n,)),
         ],
@@ -467,9 +503,16 @@
     )(
         query_states[0], key_states[0], value_states[0],
         grad_output.reshape(across_y, block_pos, width),
-        branch_gate.reshape(1, width), out_weight,
-    )
-    return dq[None], dk[None], dv[None], gate.reshape(width)
+        branch_gate, out_weight,
+    )
+    final = jax.ShapeDtypeStruct((1, positions, width), bf16)
+    return pl.pallas_call(
+        hand_over,
+        out_shape=(final, final, final, jax.ShapeDtypeStruct((width,), f32)),
+        in_specs=[anywhere] * 3 + [vmem],
+        out_specs=(anywhere,) * 3 + (vmem,),
+        scratch_shapes=[pltpu.VMEM((3, positions, width), bf16), dma((3,)), dma((3,))],
+    )(dq, dk, dv, gate)
 
 
 def solution(mesh):

time: 70.7 us -> 67.4 us (0.953)
  local copies, waits for them, and re-layouts: 5.5 us -> 0 us
  Pallas kernels: 62.9 us -> 65.8 us
    unnamed x9 -> x0, local copies, waits for them, and re-layouts: 4.21 us -> none
    pallas_call x0 -> x1, Pallas kernels: none -> 3.2 us  [per_device(): pl.pallas_call(hand_over, out_shape=(final, final, final, jax.ShapeDtypeS...]
    reshape x1 -> x0, local copies, waits for them, and re-layouts: 1.29 us -> none  [per_device(): branch_gate.reshape(1, width)]
where the time goes in v3:
time: 67.4 us; the launch traced here: 66.4 us
  Pallas kernels  65.8 us (98%)
    pallas_call x1, Pallas kernels, per_device(): pl.pallas_call(functools.partial(fused_kernel, across_x, across_y, block_...  62.6 us
    pallas_call x1, Pallas kernels, per_device(): pl.pallas_call(hand_over, out_shape=(final, final, final, jax.ShapeDtypeS...  3.2 us

profile of v3, /device:TPU:28, one launch (start us, length us, event | category | flops | bytes accessed | tf_op | source)
XLA Modules:
  0.0 66.4 jit_solution(6807244537174002932)
XLA Ops:
  0.6 62.6 %shard_map.93 = (bf16[128,1152]{1,0:T(8,128)(2,1)}, bf16[128,1152]{1,0:T(8,128)(2,1)}, bf16[128,1152]{1,0:T(8,128)(2,1)}, f32[1,1152]{1,0:T(1,128)}) custom-call(bf16[128,1152]{1,0:T(8,128)(2,1)} %bitcast.4, bf16[128,1152]{1,0:T(8,128)(2,1)} %bitcast.5, bf16[128,1152]{1,0:T(8,128)(2,1)} %bitcast.6, bf16[2,64,1152]{2,1,0:T(8,128)(2,1)} %bitcast.7, ...), custom_call_target="tpu_custom_call" | custom-call | tf_op jit(solution)/shard_map/pallas_call | solution.py:474
  63.2 3.2 %shard_map.94 = (bf16[1,128,1152]{2,1,0:T(8,128)(2,1)}, bf16[1,128,1152]{2,1,0:T(8,128)(2,1)}, bf16[1,128,1152]{2,1,0:T(8,128)(2,1)}, f32[1152]{0:T(1024)}) custom-call(bf16[128,1152]{1,0:T(8,128)(2,1)} %get-tuple-element.8.dq_in, bf16[128,1152]{1,0:T(8,128)(2,1)} %get-tuple-element.9.dk_in, bf16[128,1152]{1,0:T(8,128)(2,1)} %get-tuple-element.10.dv_in, ...), custom_call_target="tpu_custom_call" | custom-call | tf_op jit(solution)/shard_map/pallas_call | solution.py:509

commit v4 on v3

--- a/solution.py
+++ b/solution.py
@@ -176,8 +176,13 @@
     def ident(d):
         return {"tx": d // across_y, "ty": d % across_y}
 
+    half = across_x // 2
+    side = mx // half * half
+
     def other(o):
-        return lax.rem(me + o, n)
+        near, i = (side, o - half * across_y) if o > half * across_y else (half - side, o - 1)
+        to = near + lax.rem(mx + i // across_y, half)
+        return to * across_y + lax.rem(my + i % across_y, across_y)
 
     def remote(src, dst, ss, sr, d):
         return pltpu.make_async_remote_copy(
@@ -459,6 +464,7 @@
         and block_pos % (LANES // rest * 16) == 0
         and n * block_pos * rest // LANES <= 2 * LANES
         and width % LANES == 0
+        and across_x % 2 == 0
     )
     if not fits:
         return per_device_plain(

time: 67.4 us -> 70.1 us (1.040)
  the two profiles are of different devices: /device:TPU:28 before, /device:TPU:0 now
where the time goes in v4:
time: 70.1 us; the launch traced here: 69.9 us
  Pallas kernels  69.3 us (99%)
    pallas_call x1, Pallas kernels, per_device(): pl.pallas_call(functools.partial(fused_kernel, across_x, across_y, block_...  66.1 us
    pallas_call x1, Pallas kernels, per_device(): pl.pallas_call(hand_over, out_shape=(final, final, final, jax.ShapeDtypeS...  3.2 us

profile of v4, /device:TPU:0, one launch (start us, length us, event | category | flops | bytes accessed | tf_op | source)
XLA Modules:
  0.0 69.9 jit_solution(7433727043485397207)
XLA Ops:
  0.6 66.1 %shard_map.93 = (bf16[128,1152]{1,0:T(8,128)(2,1)}, bf16[128,1152]{1,0:T(8,128)(2,1)}, bf16[128,1152]{1,0:T(8,128)(2,1)}, f32[1,1152]{1,0:T(1,128)}) custom-call(bf16[128,1152]{1,0:T(8,128)(2,1)} %bitcast.4, bf16[128,1152]{1,0:T(8,128)(2,1)} %bitcast.5, bf16[128,1152]{1,0:T(8,128)(2,1)} %bitcast.6, bf16[2,64,1152]{2,1,0:T(8,128)(2,1)} %bitcast.7, ...), custom_call_target="tpu_custom_call" | custom-call | tf_op jit(solution)/shard_map/pallas_call | solution.py:480
  66.7 3.2 %shard_map.94 = (bf16[1,128,1152]{2,1,0:T(8,128)(2,1)}, bf16[1,128,1152]{2,1,0:T(8,128)(2,1)}, bf16[1,128,1152]{2,1,0:T(8,128)(2,1)}, f32[1152]{0:T(1024)}) custom-call(bf16[128,1152]{1,0:T(8,128)(2,1)} %get-tuple-element.8.dq_in, bf16[128,1152]{1,0:T(8,128)(2,1)} %get-tuple-element.9.dk_in, bf16[128,1152]{1,0:T(8,128)(2,1)} %get-tuple-element.10.dv_in, ...), custom_call_target="tpu_custom_call" | custom-call | tf_op jit(solution)/shard_map/pallas_call | solution.py:515
